TPU v7x, 32 devices: a whole 2x2x4 slice. The times are simulated.
32 devices in a mesh: gx: 4 (over y, x), gy: 2 (over core), gz: 4 (over z).
Axes of the slice: x: 2, y: 2, z: 4, core: 2. Of those that a mesh axis runs over, the one named last changes fastest.
Arguments:
- old_pos: float32 [3, 4, 2, 4, 1536], P(None, 'gx', 'gy', 'gz'), may hold values from -6 to 6
- displacement: float32 [3, 4, 2, 4, 1536], P(None, 'gx', 'gy', 'gz'), may hold values from -0.3 to 0.3
- inv_mass: float32 [4, 2, 4, 1536], P('gx', 'gy', 'gz'), may hold values from 0.0625 to 1
- bond_head: int32 [4, 2, 4, 1024], P('gx', 'gy', 'gz'), may hold values from 0 to 1535, as said below
- bond_tail: int32 [4, 2, 4, 1024], P('gx', 'gy', 'gz'), may hold values from 0 to 1967, as said below
- send_list: int32 [4, 2, 4, 16], P('gx', 'gy', 'gz'), may hold values from 0 to 1535, as said below
Outputs:
- new_pos: float32 [3, 4, 2, 4, 1536], P(None, 'gx', 'gy', 'gz')
- multipliers: float32 [4, 2, 4, 1024], P('gx', 'gy', 'gz')
Inputs may be any that keep to these rules, and one draw needn't show every extreme that they name: `bond_head`: distinct atoms of the owning domain; no atom is the first atom of two constraints. `bond_tail`: below 1536: an atom of the owning domain other than the constraint's first atom, never in send_list; otherwise a slot 1536 + block * 16 + entry with block in 0..26 other than 13, distinct within a domain; 192 constraints of each domain use such slots. `send_list`: distinct atoms of the domain; a send atom is never a constraint's first atom and never a local second atom.
All inputs are finite; a program needn't handle non-finite values.
Results may differ from a plain program's by a relative error of at most 0.0011.
Values sent between devices are 32-bit elements; how exact they have to be, the bound alone decides.
A program may use at most 64 MiB of HBM per device.

v0:
```python
import jax
import jax.numpy as jnp
from jax import lax
from jax.sharding import PartitionSpec as P

ORDER = 4


def with_halo(value, sides, width):
    for axis, dim in sides:
        devices, length = (lax.axis_size(axis), value.shape[dim])
        up = [(i, (i + 1) % devices) for i in range(devices)]
        down = [(j, i) for i, j in up]
        last = lax.slice_in_dim(value, length - width, length, axis=dim)
        leading = lax.slice_in_dim(value, 0, width, axis=dim)
        before = lax.ppermute(last, axis, up)
        after = lax.ppermute(leading, axis, down)
        value = jnp.concatenate([before, value, after], axis=dim)
    return value


def gather_back(returned):
    widened = with_halo(returned, (("gx", 1), ("gy", 2), ("gz", 3)), 1)
    return jnp.sum(widened[:, ::2, ::2, ::2, :], axis=(1, 2, 3))


def per_device(old_pos, displacement, inv_mass, bond_head, bond_tail, send_list):
    atom_count = old_pos.shape[-1]
    bond_count = bond_head.shape[-1]
    send_count = send_list.shape[-1]
    old_local = old_pos.reshape(3, atom_count)
    move_local = displacement.reshape(3, atom_count)
    mass_local = inv_mass.reshape(1, atom_count)
    head_atom = bond_head.reshape(bond_count)
    tail_atom = bond_tail.reshape(bond_count)
    outbound = send_list.reshape(send_count)
    wide_count = 27 * send_count
    packed = jnp.concatenate(
        [old_local[:, outbound], move_local[:, outbound], mass_local[:, outbound]], axis=0
    )
    arrived = with_halo(
        packed.reshape(7, 1, 1, 1, send_count), (("gx", 1), ("gy", 2), ("gz", 3)), 1
    )
    arrived = arrived.reshape(7, wide_count)
    pos_local = old_local + move_local
    ext_old = jnp.concatenate([old_local, arrived[0:3]], axis=1)
    ext_new = jnp.concatenate([pos_local, arrived[0:3] + arrived[3:6]], axis=1)
    ext_mass = jnp.concatenate([mass_local, arrived[6:7]], axis=1)
    bond_old = ext_old[:, head_atom] - ext_old[:, tail_atom]
    length = jnp.maximum(jnp.sqrt(jnp.sum(bond_old * bond_old, axis=0)), 0.5)
    direction = bond_old / length
    bond_scale = 1.0 / jnp.sqrt(ext_mass[0, head_atom] + ext_mass[0, tail_atom])

    def spread(values):
        weighted = bond_scale * values * direction
        buffer = jnp.zeros((3, atom_count + wide_count), jnp.float32)
        buffer = buffer.at[:, head_atom].add(weighted).at[:, tail_atom].add(-weighted)
        incoming = gather_back(buffer[:, atom_count:].reshape(3, 3, 3, 3, send_count))
        local_sum = buffer[:, :atom_count].at[:, outbound].add(incoming)
        return mass_local * local_sum

    def couple(values):
        shift_vec = spread(values)
        remote = with_halo(
            shift_vec[:, outbound].reshape(3, 1, 1, 1, send_count),
            (("gx", 1), ("gy", 2), ("gz", 3)),
            1,
        )
        extended = jnp.concatenate([shift_vec, remote.reshape(3, wide_count)], axis=1)
        return values - bond_scale * jnp.sum(
            direction * (extended[:, head_atom] - extended[:, tail_atom]), axis=0
        )

    def expand(right_side):
        solution = right_side
        series = right_side
        for sweep in range(ORDER):
            series = couple(series)
            solution = solution + series
        return solution

    right_one = bond_scale * (
        jnp.sum(direction * (ext_new[:, head_atom] - ext_new[:, tail_atom]), axis=0) - length
    )
    sol_one = expand(right_one)
    pos_local = pos_local - spread(sol_one)
    moved = with_halo(
        pos_local[:, outbound].reshape(3, 1, 1, 1, send_count), (("gx", 1), ("gy", 2), ("gz", 3)), 1
    )
    ext_moved = jnp.concatenate([pos_local, moved.reshape(3, wide_count)], axis=1)
    stretch = ext_moved[:, head_atom] - ext_moved[:, tail_atom]
    current = jnp.sum(stretch * stretch, axis=0)
    target = jnp.sqrt(jnp.maximum(2.0 * length * length - current, 0.5 * length * length))
    sol_two = expand(bond_scale * (length - target))
    pos_local = pos_local - spread(sol_two)
    return (pos_local.reshape(old_pos.shape), (sol_one + sol_two).reshape(bond_head.shape))


def solution(mesh):
    return jax.shard_map(
        per_device,
        mesh=mesh,
        in_specs=(
            P(None, "gx", "gy", "gz", None),
            P(None, "gx", "gy", "gz", None),
            P("gx", "gy", "gz", None),
            P("gx", "gy", "gz", None),
            P("gx", "gy", "gz", None),
            P("gx", "gy", "gz", None),
        ),
        out_specs=(P(None, "gx", "gy", "gz", None), P("gx", "gy", "gz", None)),
        check_vma=False,
    )
```

profile of v0, /device:TPU:0, one launch (start us, length us, event | category | flops | bytes accessed | tf_op | source)
XLA Modules:
  0.0 540.6 jit_solution(5825422829706087112)
XLA Ops:
  33.9 6.5 %gather_fusion.4 = f32[1024]{0:T(1024)S(1)} fusion(f32[1,1968]{1,0:T(1,128)S(1)} %pad_maximum_fusion.83, s32[1024]{0:T(1024)S(1)} %bitcast.84), kind=kCustom, calls=%fused_computation.4 | custom fusion | bytes 16384 | tf_op jit(solution)/shard_map/gather | solution.py:52
  40.4 6.5 %gather_fusion.3 = f32[1024]{0:T(1024)S(1)} fusion(f32[1,1968]{1,0:T(1,128)S(1)} %pad_maximum_fusion.83, s32[1024]{0:T(1024)S(1)} %bitcast.85), kind=kCustom, calls=%fused_computation.3 | custom fusion | bytes 16384 | tf_op jit(solution)/shard_map/gather | solution.py:52
  48.5 6.9 %scatter_custom_fusion = f32[3,1968]{0,1:T(8,128)S(1)} fusion(s32[1024]{0:T(1024)S(1)} %bitcast.184, f32[]{:T(128)} %constant.6.clone.1, f32[1024]{0:T(1024)S(1)} %get-tuple-element.18, f32[1024,3]{1,0:T(8,128)S(1)} %get-tuple-element.22, f32[1024]{0:T(1024)S(1)} %sqrt_maximum_fusion), kind=kCustom, calls=%fused_computation.128 | custom fusion | flops 9216 | bytes 556100 | tf_op jit(solution)/shard_map/scatter-add | solution.py:57
  55.4 7.1 %scatter_custom_fusion.1 = f32[3,1968]{0,1:T(8,128)S(1)} fusion(f32[3,1968]{0,1:T(8,128)S(1)} %scatter_custom_fusion, s32[1024]{0:T(1024)S(1)} %bitcast.173, f32[1024]{0:T(1024)S(1)} %get-tuple-element.18, f32[1024,3]{1,0:T(8,128)S(1)} %get-tuple-element.22, f32[1024]{0:T(1024)S(1)} %sqrt_maximum_fusion), kind=kCustom, calls=%fused_computation.97 | custom fusion | flops 12288 | bytes 556096 | tf_op jit(solution)/shard_map/scatter-add | solution.py:57
  100.4 6.9 %scatter_custom_fusion.3 = f32[3,1968]{0,1:T(8,128)S(1)} fusion(s32[1024]{0:T(1024)S(1)} %bitcast.185, f32[]{:T(128)} %constant.6.clone.1, f32[1024]{0:T(1024)S(1)} %fusion.89, f32[1024,3]{1,0:T(8,128)S(1)} %get-tuple-element.22, f32[1024]{0:T(1024)S(1)} %sqrt_maximum_fusion), kind=kCustom, calls=%fused_computation.126 | custom fusion | flops 9216 | bytes 556100 | tf_op jit(solution)/shard_map/scatter-add | solution.py:57
  107.4 7.1 %scatter_custom_fusion.4 = f32[3,1968]{0,1:T(8,128)S(1)} fusion(f32[3,1968]{0,1:T(8,128)S(1)} %scatter_custom_fusion.3, s32[1024]{0:T(1024)S(1)} %bitcast.174, f32[1024]{0:T(1024)S(1)} %fusion.89, f32[1024,3]{1,0:T(8,128)S(1)} %get-tuple-element.22, f32[1024]{0:T(1024)S(1)} %sqrt_maximum_fusion), kind=kCustom, calls=%fused_computation.95 | custom fusion | flops 12288 | bytes 556096 | tf_op jit(solution)/shard_map/scatter-add | solution.py:57
  147.2 4.0 gather_fusion.13
  151.6 6.9 %scatter_custom_fusion.6 = f32[3,1968]{0,1:T(8,128)S(1)} fusion(s32[1024]{0:T(1024)S(1)} %bitcast.186, f32[]{:T(128)} %constant.6.clone.1, f32[1024]{0:T(1024)S(1)} %fusion.92, f32[1024,3]{1,0:T(8,128)S(1)} %get-tuple-element.22, f32[1024]{0:T(1024)S(1)} %sqrt_maximum_fusion), kind=kCustom, calls=%fused_computation.124 | custom fusion | flops 9216 | bytes 556100 | tf_op jit(solution)/shard_map/scatter-add | solution.py:57
  158.6 7.3 %scatter_custom_fusion.7 = f32[3,1968]{0,1:T(8,128)S(1)} fusion(f32[3,1968]{0,1:T(8,128)S(1)} %scatter_custom_fusion.6, s32[1024]{0:T(1024)S(1)} %bitcast.175, f32[1024]{0:T(1024)S(1)} %fusion.92, f32[1024,3]{1,0:T(8,128)S(1)} %get-tuple-element.22, f32[1024]{0:T(1024)S(1)} %sqrt_maximum_fusion), kind=kCustom, calls=%fused_computation.93 | custom fusion | flops 12288 | bytes 556096 | tf_op jit(solution)/shard_map/scatter-add | solution.py:57
  203.9 6.9 %scatter_custom_fusion.9 = f32[3,1968]{0,1:T(8,128)S(1)} fusion(s32[1024]{0:T(1024)S(1)} %bitcast.187, f32[]{:T(128)} %constant.6.clone.1, f32[1024]{0:T(1024)S(1)} %fusion.87, f32[1024,3]{1,0:T(8,128)S(1)} %get-tuple-element.22, f32[1024]{0:T(1024)S(1)} %sqrt_maximum_fusion), kind=kCustom, calls=%fused_computation.122 | custom fusion | flops 9216 | bytes 556100 | tf_op jit(solution)/shard_map/scatter-add | solution.py:57
  210.8 7.1 %scatter_custom_fusion.10 = f32[3,1968]{0,1:T(8,128)S(1)} fusion(f32[3,1968]{0,1:T(8,128)S(1)} %scatter_custom_fusion.9, s32[1024]{0:T(1024)S(1)} %bitcast.176, f32[1024]{0:T(1024)S(1)} %fusion.87, f32[1024,3]{1,0:T(8,128)S(1)} %get-tuple-element.22, f32[1024]{0:T(1024)S(1)} %sqrt_maximum_fusion), kind=kCustom, calls=%fused_computation.91 | custom fusion | flops 12288 | bytes 556096 | tf_op jit(solution)/shard_map/scatter-add | solution.py:57
  250.5 4.0 gather_fusion.19
  255.0 6.9 %scatter_custom_fusion.12 = f32[3,1968]{0,1:T(8,128)S(1)} fusion(s32[1024]{0:T(1024)S(1)} %bitcast.188, f32[]{:T(128)} %constant.6.clone.1, f32[1024]{0:T(1024)S(1)} %add_multiply_fusion.1, f32[1024,3]{1,0:T(8,128)S(1)} %get-tuple-element.22, f32[1024]{0:T(1024)S(1)} %sqrt_maximum_fusion), kind=kCustom, calls=%fused_computation.120 | custom fusion | flops 9216 | bytes 556100 | tf_op jit(solution)/shard_map/scatter-add | solution.py:57
  261.9 7.1 %scatter_custom_fusion.13 = f32[3,1968]{0,1:T(8,128)S(1)} fusion(f32[3,1968]{0,1:T(8,128)S(1)} %scatter_custom_fusion.12, s32[1024]{0:T(1024)S(1)} %bitcast.177, f32[1024]{0:T(1024)S(1)} %add_multiply_fusion.1, f32[1024,3]{1,0:T(8,128)S(1)} %get-tuple-element.22, f32[1024]{0:T(1024)S(1)} %sqrt_maximum_fusion), kind=kCustom, calls=%fused_computation.89 | custom fusion | flops 12288 | bytes 556096 | tf_op jit(solution)/shard_map/scatter-add | solution.py:57
  308.8 6.9 %scatter_custom_fusion.15 = f32[3,1968]{0,1:T(8,128)S(1)} fusion(s32[1024]{0:T(1024)S(1)} %bitcast.189, f32[]{:T(128)} %constant.6.clone.1, f32[1024]{0:T(1024)S(1)} %get-tuple-element.16, f32[1024,3]{1,0:T(8,128)S(1)} %get-tuple-element.22, f32[1024]{0:T(1024)S(1)} %sqrt_maximum_fusion), kind=kCustom, calls=%fused_computation.118 | custom fusion | flops 9216 | bytes 556100 | tf_op jit(solution)/shard_map/scatter-add | solution.py:57
  315.7 7.3 %scatter_custom_fusion.16 = f32[3,1968]{0,1:T(8,128)S(1)} fusion(f32[3,1968]{0,1:T(8,128)S(1)} %scatter_custom_fusion.15, s32[1024]{0:T(1024)S(1)} %bitcast.178, f32[1024]{0:T(1024)S(1)} %get-tuple-element.16, f32[1024,3]{1,0:T(8,128)S(1)} %get-tuple-element.22, f32[1024]{0:T(1024)S(1)} %sqrt_maximum_fusion), kind=kCustom, calls=%fused_computation.87 | custom fusion | flops 12288 | bytes 556096 | tf_op jit(solution)/shard_map/scatter-add | solution.py:57
  358.8 6.9 %scatter_custom_fusion.18 = f32[3,1968]{0,1:T(8,128)S(1)} fusion(s32[1024]{0:T(1024)S(1)} %bitcast.190, f32[]{:T(128)} %constant.6.clone.1, f32[1024]{0:T(1024)S(1)} %fusion.90, f32[1024,3]{1,0:T(8,128)S(1)} %get-tuple-element.22, f32[1024]{0:T(1024)S(1)} %sqrt_maximum_fusion), kind=kCustom, calls=%fused_computation.116 | custom fusion | flops 9216 | bytes 556100 | tf_op jit(solution)/shard_map/scatter-add | solution.py:57
  365.7 7.1 %scatter_custom_fusion.19 = f32[3,1968]{0,1:T(8,128)S(1)} fusion(f32[3,1968]{0,1:T(8,128)S(1)} %scatter_custom_fusion.18, s32[1024]{0:T(1024)S(1)} %bitcast.179, f32[1024]{0:T(1024)S(1)} %fusion.90, f32[1024,3]{1,0:T(8,128)S(1)} %get-tuple-element.22, f32[1024]{0:T(1024)S(1)} %sqrt_maximum_fusion), kind=kCustom, calls=%fused_computation.85 | custom fusion | flops 12288 | bytes 556096 | tf_op jit(solution)/shard_map/scatter-add | solution.py:57
  409.6 6.9 %scatter_custom_fusion.21 = f32[3,1968]{0,1:T(8,128)S(1)} fusion(s32[1024]{0:T(1024)S(1)} %bitcast.191, f32[]{:T(128)} %constant.6.clone.1, f32[1024]{0:T(1024)S(1)} %fusion.93, f32[1024,3]{1,0:T(8,128)S(1)} %get-tuple-element.22, f32[1024]{0:T(1024)S(1)} %sqrt_maximum_fusion), kind=kCustom, calls=%fused_computation.114 | custom fusion | flops 9216 | bytes 556100 | tf_op jit(solution)/shard_map/scatter-add | solution.py:57
  416.5 7.1 %scatter_custom_fusion.22 = f32[3,1968]{0,1:T(8,128)S(1)} fusion(f32[3,1968]{0,1:T(8,128)S(1)} %scatter_custom_fusion.21, s32[1024]{0:T(1024)S(1)} %bitcast.180, f32[1024]{0:T(1024)S(1)} %fusion.93, f32[1024,3]{1,0:T(8,128)S(1)} %get-tuple-element.22, f32[1024]{0:T(1024)S(1)} %sqrt_maximum_fusion), kind=kCustom, calls=%fused_computation.83 | custom fusion | flops 12288 | bytes 556096 | tf_op jit(solution)/shard_map/scatter-add | solution.py:57
  459.6 6.9 %scatter_custom_fusion.24 = f32[3,1968]{0,1:T(8,128)S(1)} fusion(s32[1024]{0:T(1024)S(1)} %bitcast.192, f32[]{:T(128)} %constant.6.clone.1, f32[1024]{0:T(1024)S(1)} %fusion.88, f32[1024,3]{1,0:T(8,128)S(1)} %get-tuple-element.22, f32[1024]{0:T(1024)S(1)} %sqrt_maximum_fusion), kind=kCustom, calls=%fused_computation.112 | custom fusion | flops 9216 | bytes 556100 | tf_op jit(solution)/shard_map/scatter-add | solution.py:57
  466.6 7.3 %scatter_custom_fusion.25 = f32[3,1968]{0,1:T(8,128)S(1)} fusion(f32[3,1968]{0,1:T(8,128)S(1)} %scatter_custom_fusion.24, s32[1024]{0:T(1024)S(1)} %bitcast.181, f32[1024]{0:T(1024)S(1)} %fusion.88, f32[1024,3]{1,0:T(8,128)S(1)} %get-tuple-element.22, f32[1024]{0:T(1024)S(1)} %sqrt_maximum_fusion), kind=kCustom, calls=%fused_computation.81 | custom fusion | flops 12288 | bytes 556096 | tf_op jit(solution)/shard_map/scatter-add | solution.py:57
  510.7 6.9 %scatter_custom_fusion.27 = f32[3,1968]{0,1:T(8,128)S(1)} fusion(s32[1024]{0:T(1024)S(1)} %bitcast.193, f32[]{:T(128)} %constant.6.clone.1, f32[1024]{0:T(1024)S(1)} %add_multiply_fusion, f32[1024,3]{1,0:T(8,128)S(1)} %get-tuple-element.22, f32[1024]{0:T(1024)S(1)} %sqrt_maximum_fusion), kind=kCustom, calls=%fused_computation.110 | custom fusion | flops 9216 | bytes 556100 | tf_op jit(solution)/shard_map/scatter-add | solution.py:57
  517.7 7.1 %scatter_custom_fusion.28 = f32[3,1968]{0,1:T(8,128)S(1)} fusion(f32[3,1968]{0,1:T(8,128)S(1)} %scatter_custom_fusion.27, s32[1024]{0:T(1024)S(1)} %bitcast.182, f32[1024]{0:T(1024)S(1)} %add_multiply_fusion, f32[1024,3]{1,0:T(8,128)S(1)} %get-tuple-element.22, f32[1024]{0:T(1024)S(1)} %sqrt_maximum_fusion), kind=kCustom, calls=%fused_computation.79 | custom fusion | flops 12288 | bytes 556096 | tf_op jit(solution)/shard_map/scatter-add | solution.py:57
  (545 shorter events, 375.9 us)
Async XLA Ops:
  4.2 5.5 %collective-permute-start = (f32[7,1,1,1,16]{4,0,3,2,1:T(8,128)S(1)}, f32[7,1,1,1,16]{4,0,3,2,1:T(8,128)S(1)}, u32[]{:S(2)}, u32[]{:S(2)}) collective-permute-start(f32[7,1,1,1,16]{4,0,3,2,1:T(8,128)S(1)} %bitcast.112), channel_id=1, source_target_pairs={{0,8},{8,16},{16,24},{24,0},{1,9},{9,17},{17,25},{25,1},{2,10},{10... | collective-permute-start | bytes 1352 | tf_op jit(solution)/shard_map/ppermute | solution.py:16
  12.1 5.9 %collective-permute-start.4 = (f32[7,3,3,1,16]{4,0,3,2,1:T(8,128)S(1)}, f32[7,3,3,1,16]{4,0,3,2,1:T(8,128)S(1)}, u32[]{:S(2)}, u32[]{:S(2)}) collective-permute-start(f32[7,3,3,1,16]{4,0,3,2,1:T(8,128)S(1)} %pad_maximum_fusion.41), channel_id=1, source_target_pairs={{0,1},{1,2},{2,3},{3,0},{4,5},{5,6},{6,7},{7,4},{8,9},{9,10},{10,1... | collective-permute-start | bytes 12104 | tf_op jit(solution)/shard_map/ppermute | solution.py:16
  70.6 5.8 %collective-permute-start.10 = (f32[3,5,5,1,16]{4,3,2,1,0:T(1,128)S(1)}, f32[3,5,5,1,16]{4,3,2,1,0:T(1,128)S(1)}, u32[]{:S(2)}, u32[]{:S(2)}) collective-permute-start(f32[3,5,5,1,16]{4,3,2,1,0:T(1,128)S(1)} %get-tuple-element.45), channel_id=1, source_target_pairs={{0,1},{1,2},{2,3},{3,0},{4,5},{5,6},{6,7},{7,4},{8,9},{9,10},{10,1... | collective-permute-start | bytes 14408 | tf_op jit(solution)/shard_map/ppermute | solution.py:16
  85.1 5.6 %collective-permute-start.16 = (f32[3,3,3,1,16]{4,0,3,2,1:T(4,128)S(1)}, f32[3,3,3,1,16]{4,0,3,2,1:T(4,128)S(1)}, u32[]{:S(2)}, u32[]{:S(2)}) collective-permute-start(f32[3,3,3,1,16]{4,0,3,2,1:T(4,128)S(1)} %pad_maximum_fusion.72), channel_id=1, source_target_pairs={{0,1},{1,2},{2,3},{3,0},{4,5},{5,6},{6,7},{7,4},{8,9},{9,10},{10,1... | collective-permute-start | bytes 5192 | tf_op jit(solution)/shard_map/ppermute | solution.py:16
  121.6 6.1 %collective-permute-start.22 = (f32[3,5,5,1,16]{4,3,2,1,0:T(1,128)S(1)}, f32[3,5,5,1,16]{4,3,2,1,0:T(1,128)S(1)}, u32[]{:S(2)}, u32[]{:S(2)}) collective-permute-start(f32[3,5,5,1,16]{4,3,2,1,0:T(1,128)S(1)} %get-tuple-element.43), channel_id=1, source_target_pairs={{0,1},{1,2},{2,3},{3,0},{4,5},{5,6},{6,7},{7,4},{8,9},{9,10},{10,1... | collective-permute-start | bytes 14408 | tf_op jit(solution)/shard_map/ppermute | solution.py:16
  122.8 4.9 collective-permute-start.23
  136.2 5.6 %collective-permute-start.28 = (f32[3,3,3,1,16]{4,0,3,2,1:T(4,128)S(1)}, f32[3,3,3,1,16]{4,0,3,2,1:T(4,128)S(1)}, u32[]{:S(2)}, u32[]{:S(2)}) collective-permute-start(f32[3,3,3,1,16]{4,0,3,2,1:T(4,128)S(1)} %pad_maximum_fusion.73), channel_id=1, source_target_pairs={{0,1},{1,2},{2,3},{3,0},{4,5},{5,6},{6,7},{7,4},{8,9},{9,10},{10,1... | collective-permute-start | bytes 5192 | tf_op jit(solution)/shard_map/ppermute | solution.py:16
  174.0 5.9 %collective-permute-start.34 = (f32[3,5,5,1,16]{4,3,2,1,0:T(1,128)S(1)}, f32[3,5,5,1,16]{4,3,2,1,0:T(1,128)S(1)}, u32[]{:S(2)}, u32[]{:S(2)}) collective-permute-start(f32[3,5,5,1,16]{4,3,2,1,0:T(1,128)S(1)} %get-tuple-element.41), channel_id=1, source_target_pairs={{0,1},{1,2},{2,3},{3,0},{4,5},{5,6},{6,7},{7,4},{8,9},{9,10},{10,1... | collective-permute-start | bytes 14408 | tf_op jit(solution)/shard_map/ppermute | solution.py:16
  188.5 5.6 %collective-permute-start.40 = (f32[3,3,3,1,16]{4,0,3,2,1:T(4,128)S(1)}, f32[3,3,3,1,16]{4,0,3,2,1:T(4,128)S(1)}, u32[]{:S(2)}, u32[]{:S(2)}) collective-permute-start(f32[3,3,3,1,16]{4,0,3,2,1:T(4,128)S(1)} %pad_maximum_fusion.74), channel_id=1, source_target_pairs={{0,1},{1,2},{2,3},{3,0},{4,5},{5,6},{6,7},{7,4},{8,9},{9,10},{10,1... | collective-permute-start | bytes 5192 | tf_op jit(solution)/shard_map/ppermute | solution.py:16
  225.0 5.9 %collective-permute-start.46 = (f32[3,5,5,1,16]{4,3,2,1,0:T(1,128)S(1)}, f32[3,5,5,1,16]{4,3,2,1,0:T(1,128)S(1)}, u32[]{:S(2)}, u32[]{:S(2)}) collective-permute-start(f32[3,5,5,1,16]{4,3,2,1,0:T(1,128)S(1)} %get-tuple-element.39), channel_id=1, source_target_pairs={{0,1},{1,2},{2,3},{3,0},{4,5},{5,6},{6,7},{7,4},{8,9},{9,10},{10,1... | collective-permute-start | bytes 14408 | tf_op jit(solution)/shard_map/ppermute | solution.py:16
  226.1 4.8 collective-permute-start.47
  239.5 5.6 %collective-permute-start.52 = (f32[3,3,3,1,16]{4,0,3,2,1:T(4,128)S(1)}, f32[3,3,3,1,16]{4,0,3,2,1:T(4,128)S(1)}, u32[]{:S(2)}, u32[]{:S(2)}) collective-permute-start(f32[3,3,3,1,16]{4,0,3,2,1:T(4,128)S(1)} %pad_maximum_fusion.75), channel_id=1, source_target_pairs={{0,1},{1,2},{2,3},{3,0},{4,5},{5,6},{6,7},{7,4},{8,9},{9,10},{10,1... | collective-permute-start | bytes 5192 | tf_op jit(solution)/shard_map/ppermute | solution.py:16
  277.1 6.3 %collective-permute-start.58 = (f32[3,5,5,1,16]{4,3,2,1,0:T(1,128)S(1)}, f32[3,5,5,1,16]{4,3,2,1,0:T(1,128)S(1)}, u32[]{:S(2)}, u32[]{:S(2)}) collective-permute-start(f32[3,5,5,1,16]{4,3,2,1,0:T(1,128)S(1)} %get-tuple-element.37), channel_id=1, source_target_pairs={{0,1},{1,2},{2,3},{3,0},{4,5},{5,6},{6,7},{7,4},{8,9},{9,10},{10,1... | collective-permute-start | bytes 14408 | tf_op jit(solution)/shard_map/ppermute | solution.py:16
  294.8 5.6 %collective-permute-start.64 = (f32[3,3,3,1,16]{4,0,3,2,1:T(4,128)S(1)}, f32[3,3,3,1,16]{4,0,3,2,1:T(4,128)S(1)}, u32[]{:S(2)}, u32[]{:S(2)}) collective-permute-start(f32[3,3,3,1,16]{4,0,3,2,1:T(4,128)S(1)} %pad_maximum_fusion.76), channel_id=1, source_target_pairs={{0,1},{1,2},{2,3},{3,0},{4,5},{5,6},{6,7},{7,4},{8,9},{9,10},{10,1... | collective-permute-start | bytes 5192 | tf_op jit(solution)/shard_map/ppermute | solution.py:16
  330.1 6.0 %collective-permute-start.70 = (f32[3,5,5,1,16]{4,3,2,1,0:T(1,128)S(1)}, f32[3,5,5,1,16]{4,3,2,1,0:T(1,128)S(1)}, u32[]{:S(2)}, u32[]{:S(2)}) collective-permute-start(f32[3,5,5,1,16]{4,3,2,1,0:T(1,128)S(1)} %get-tuple-element.35), channel_id=1, source_target_pairs={{0,1},{1,2},{2,3},{3,0},{4,5},{5,6},{6,7},{7,4},{8,9},{9,10},{10,1... | collective-permute-start | bytes 14408 | tf_op jit(solution)/shard_map/ppermute | solution.py:16
  331.2 4.8 collective-permute-start.71
  344.6 5.6 %collective-permute-start.76 = (f32[3,3,3,1,16]{4,0,3,2,1:T(4,128)S(1)}, f32[3,3,3,1,16]{4,0,3,2,1:T(4,128)S(1)}, u32[]{:S(2)}, u32[]{:S(2)}) collective-permute-start(f32[3,3,3,1,16]{4,0,3,2,1:T(4,128)S(1)} %pad_maximum_fusion.77), channel_id=1, source_target_pairs={{0,1},{1,2},{2,3},{3,0},{4,5},{5,6},{6,7},{7,4},{8,9},{9,10},{10,1... | collective-permute-start | bytes 5192 | tf_op jit(solution)/shard_map/ppermute | solution.py:16
  380.9 6.0 %collective-permute-start.82 = (f32[3,5,5,1,16]{4,3,2,1,0:T(1,128)S(1)}, f32[3,5,5,1,16]{4,3,2,1,0:T(1,128)S(1)}, u32[]{:S(2)}, u32[]{:S(2)}) collective-permute-start(f32[3,5,5,1,16]{4,3,2,1,0:T(1,128)S(1)} %get-tuple-element.33), channel_id=1, source_target_pairs={{0,1},{1,2},{2,3},{3,0},{4,5},{5,6},{6,7},{7,4},{8,9},{9,10},{10,1... | collective-permute-start | bytes 14408 | tf_op jit(solution)/shard_map/ppermute | solution.py:16
  395.4 5.6 %collective-permute-start.88 = (f32[3,3,3,1,16]{4,0,3,2,1:T(4,128)S(1)}, f32[3,3,3,1,16]{4,0,3,2,1:T(4,128)S(1)}, u32[]{:S(2)}, u32[]{:S(2)}) collective-permute-start(f32[3,3,3,1,16]{4,0,3,2,1:T(4,128)S(1)} %pad_maximum_fusion.78), channel_id=1, source_target_pairs={{0,1},{1,2},{2,3},{3,0},{4,5},{5,6},{6,7},{7,4},{8,9},{9,10},{10,1... | collective-permute-start | bytes 5192 | tf_op jit(solution)/shard_map/ppermute | solution.py:16
  430.7 6.2 %collective-permute-start.94 = (f32[3,5,5,1,16]{4,3,2,1,0:T(1,128)S(1)}, f32[3,5,5,1,16]{4,3,2,1,0:T(1,128)S(1)}, u32[]{:S(2)}, u32[]{:S(2)}) collective-permute-start(f32[3,5,5,1,16]{4,3,2,1,0:T(1,128)S(1)} %get-tuple-element.31), channel_id=1, source_target_pairs={{0,1},{1,2},{2,3},{3,0},{4,5},{5,6},{6,7},{7,4},{8,9},{9,10},{10,1... | collective-permute-start | bytes 14408 | tf_op jit(solution)/shard_map/ppermute | solution.py:16
  445.5 5.6 %collective-permute-start.100 = (f32[3,3,3,1,16]{4,0,3,2,1:T(4,128)S(1)}, f32[3,3,3,1,16]{4,0,3,2,1:T(4,128)S(1)}, u32[]{:S(2)}, u32[]{:S(2)}) collective-permute-start(f32[3,3,3,1,16]{4,0,3,2,1:T(4,128)S(1)} %pad_maximum_fusion.79), channel_id=1, source_target_pairs={{0,1},{1,2},{2,3},{3,0},{4,5},{5,6},{6,7},{7,4},{8,9},{9,10},{10,1... | collective-permute-start | bytes 5192 | tf_op jit(solution)/shard_map/ppermute | solution.py:16
  482.0 6.0 %collective-permute-start.106 = (f32[3,5,5,1,16]{4,3,2,1,0:T(1,128)S(1)}, f32[3,5,5,1,16]{4,3,2,1,0:T(1,128)S(1)}, u32[]{:S(2)}, u32[]{:S(2)}) collective-permute-start(f32[3,5,5,1,16]{4,3,2,1,0:T(1,128)S(1)} %get-tuple-element.29), channel_id=1, source_target_pairs={{0,1},{1,2},{2,3},{3,0},{4,5},{5,6},{6,7},{7,4},{8,9},{9,10},{10,1... | collective-permute-start | bytes 14408 | tf_op jit(solution)/shard_map/ppermute | solution.py:16
  496.6 5.6 %collective-permute-start.112 = (f32[3,3,3,1,16]{4,0,3,2,1:T(4,128)S(1)}, f32[3,3,3,1,16]{4,0,3,2,1:T(4,128)S(1)}, u32[]{:S(2)}, u32[]{:S(2)}) collective-permute-start(f32[3,3,3,1,16]{4,0,3,2,1:T(4,128)S(1)} %pad_maximum_fusion.80), channel_id=1, source_target_pairs={{0,1},{1,2},{2,3},{3,0},{4,5},{5,6},{6,7},{7,4},{8,9},{9,10},{10,1... | collective-permute-start | bytes 5192 | tf_op jit(solution)/shard_map/ppermute | solution.py:16
  531.9 6.0 %collective-permute-start.118 = (f32[3,5,5,1,16]{4,3,2,1,0:T(1,128)S(1)}, f32[3,5,5,1,16]{4,3,2,1,0:T(1,128)S(1)}, u32[]{:S(2)}, u32[]{:S(2)}) collective-permute-start(f32[3,5,5,1,16]{4,3,2,1,0:T(1,128)S(1)} %get-tuple-element.27), channel_id=1, source_target_pairs={{0,1},{1,2},{2,3},{3,0},{4,5},{5,6},{6,7},{7,4},{8,9},{9,10},{10,1... | collective-permute-start | bytes 14408 | tf_op jit(solution)/shard_map/ppermute | solution.py:16
  (104 other events, 305.3 us)
where the time goes:
time: 549 us; the launch traced here: 541 us
  other arithmetic  173 us (32%)
  starting transfers between devices  149 us (27%)
  local copies, waits for them, and re-layouts  114 us (21%)
  waiting for transfers between devices  101 us (18%)
    scatter-add x20, other arithmetic, spread(): buffer.at[:, head_atom].add(weighted).at[:, tail_atom].add(-weighted)  141 us
    ppermute x60, starting transfers between devices, with_halo(): after = lax.ppermute(leading, axis, down)  88.1 us
    ppermute x60, waiting for transfers between devices, with_halo(): before = lax.ppermute(last, axis, up)  80.8 us
    ppermute x60, starting transfers between devices, with_halo(): before = lax.ppermute(last, axis, up)  61.3 us
    gather x8, local copies, waits for them, and re-layouts, couple(): extended[:, head_atom] - extended[:, tail_atom]  32.1 us
    gather x8, local copies, waits for them, and re-layouts, couple(): extended[:, tail_atom]  27.3 us
    ppermute x60, waiting for transfers between devices, with_halo(): after = lax.ppermute(leading, axis, down)  19.9 us
    gather x2, local copies, waits for them, and re-layouts, per_device(): bond_scale = 1.0 / jnp.sqrt(ext_mass[0, head_atom] + ext_mass[0, tail_atom])  12.9 us
  transfers between devices with their start and end apart: 120, of which 103 were waited for; matrix products, arithmetic and copies ran while one was open for 1% of the time, Pallas kernels for 0%

commit v1 on v0

v1 whole, which is shorter than its diff:
```python
import functools
import itertools

import jax
import jax.numpy as jnp
from jax import lax
from jax.experimental import pallas as pl
from jax.experimental.pallas import tpu as pltpu
from jax.sharding import PartitionSpec as P

ORDER = 4
LANES = 128
F32, BF16 = jnp.float32, jnp.bfloat16
MESH = pl.DeviceIdType.MESH


def pieces(value):
    high = value.astype(BF16).astype(F32)
    rest = value - high
    middle = rest.astype(BF16).astype(F32)
    return jnp.concatenate([high, middle, rest - middle], axis=0).astype(BF16)


def fold(out):
    rows = out.shape[0] // 3
    return out[:rows] + out[rows : 2 * rows] + out[2 * rows :]


def dot_nt(left, right):
    return lax.dot_general(left, right, (((1,), (1,)), ((), ())), preferred_element_type=F32)


def dot_nn(left, right):
    return lax.dot_general(left, right, (((1,), (0,)), ((), ())), preferred_element_type=F32)


def rows8(parts):
    count = sum(part.shape[0] for part in parts)
    pad = -count % 8
    if pad:
        parts = list(parts) + [jnp.zeros((pad, parts[0].shape[1]), F32)]
    return jnp.concatenate(parts, axis=0)


def plan(sizes, send_count):
    groups = LANES // send_count
    entries = []
    for block in range(27):
        off = (block // 9 - 1, block // 3 % 3 - 1, block % 3 - 1)
        if off == (0, 0, 0):
            continue
        canon = tuple(o % n for o, n in zip(off, sizes))
        for where, blocks in entries:
            if where == canon and all((b - block) % groups for b in blocks):
                blocks.append(block)
                break
        else:
            entries.append((canon, [block]))
    return entries


def kernel(
    axes, sizes, send_count,
    old_ref, move_ref, mass_ref, head_ref, tail_ref, send_ref,
    pos_ref, mult_ref,
    hot, pick, a_high, a_low, col,
    out0, in0, out1, in1, out2, in2, out3, in3, out4, in4,
    send_sem, recv_sem,
):
    atoms = old_ref.shape[-1]
    bonds = head_ref.shape[-1]
    groups = LANES // send_count
    slot_tiles = -(-27 // groups)
    slots = slot_tiles * LANES
    entries = plan(sizes, send_count)
    devices = []
    for where, _ in entries:
        if where != (0, 0, 0) and where not in devices:
            devices.append(where)
    here = [lax.axis_index(name) for name in axes]

    def target(where):
        return tuple(lax.rem(i + o, n) for i, o, n in zip(here, where, sizes))

    barrier = pltpu.get_barrier_semaphore()
    for where in devices:
        pl.semaphore_signal(barrier, inc=1, device_id=target(where), device_id_type=MESH)

    send_row = jnp.concatenate(
        [send_ref[0, 0].astype(F32), jnp.zeros((1, LANES - send_count), F32)], axis=1
    )
    send_rep = jnp.broadcast_to(send_row, (8, LANES))
    shift = send_count
    while shift < LANES:
        send_rep = send_rep + pltpu.roll(send_rep, shift, 1)
        shift *= 2
    send_col = send_rep.T[:, 0:1]
    atom_lane = lax.broadcasted_iota(jnp.int32, (1, atoms), 1).astype(F32)
    pick[...] = jnp.where(send_col == atom_lane, 1.0, 0.0).astype(BF16)

    old = jnp.concatenate([old_ref[k, 0, 0] for k in range(3)], axis=0)
    pos0 = old + jnp.concatenate([move_ref[k, 0, 0] for k in range(3)], axis=0)
    mass = mass_ref[0, 0]
    values = pieces(rows8([old, pos0, mass]))
    out0[...] = fold(dot_nt(values, pick[...]))

    if devices:
        pl.semaphore_wait(barrier, len(devices))

    def copies_same(step, source, landing):
        started = []
        for i, where in enumerate(devices):
            copy = pltpu.make_async_remote_copy(
                source, landing.at[i], send_sem.at[step, i], recv_sem.at[step, i],
                device_id=target(where), device_id_type=MESH,
            )
            copy.start()
            started.append(copy)
        return started

    def copies_each(step, source, landing):
        started = []
        for i, (where, _) in enumerate(entries):
            if where == (0, 0, 0):
                landing[i] = source[i]
                continue
            copy = pltpu.make_async_remote_copy(
                source.at[i], landing.at[i], send_sem.at[step, i], recv_sem.at[step, i],
                device_id=target(where), device_id_type=MESH,
            )
            copy.start()
            started.append(copy)
        return started

    pending = []

    def arrive(started):
        for copy in started:
            copy.wait_recv()
        pending.extend(started)

    lane_group = lax.broadcasted_iota(jnp.int32, (1, LANES), 1) // send_count

    def view(own, landing):
        tiles = []
        for q in range(slot_tiles):
            tile = jnp.zeros(own.shape, F32)
            for block in range(q * groups, min(27, (q + 1) * groups)):
                if block == 13:
                    continue
                off = (block // 9 - 1, block // 3 % 3 - 1, block % 3 - 1)
                back = tuple(-o % n for o, n in zip(off, sizes))
                data = own[...] if back == (0, 0, 0) else landing[devices.index(back)]
                tile = jnp.where(lane_group == block % groups, data, tile)
            tiles.append(tile)
        return jnp.concatenate(tiles, axis=1)

    def fill(source, rows):
        for i, (_, blocks) in enumerate(entries):
            tile = jnp.zeros((rows.shape[0], LANES), F32)
            for block in blocks:
                q = block // groups
                tile = jnp.where(
                    lane_group == block % groups, rows[:, q * LANES : (q + 1) * LANES], tile
                )
            source[i] = tile

    first = copies_same(0, out0, in0)

    head = head_ref[0, 0].astype(F32)
    tail = tail_ref[0, 0].astype(F32)
    col[...] = rows8([head, tail]).T
    wide_lane = lax.broadcasted_iota(jnp.int32, (1, atoms + slots), 1).astype(F32)
    step_rows = 16

    def hot_rows(i, carry):
        base = pl.multiple_of(i * step_rows, step_rows)
        block = col[pl.ds(base, step_rows), :]
        hot[pl.ds(base, step_rows), :] = jnp.where(block[:, 0:1] == wide_lane, 1.0, 0.0).astype(BF16)
        hot[pl.ds(bonds + base, step_rows), :] = jnp.where(
            block[:, 1:2] == wide_lane, 1.0, 0.0
        ).astype(BF16)
        return carry

    lax.fori_loop(0, bonds // step_rows, hot_rows, 0)
    ends = fold(dot_nt(values, hot[:, :atoms]))

    arrive(first)
    far = fold(dot_nt(pieces(view(out0, in0)), hot[bonds:, atoms:]))
    at_head = ends[:, :bonds]
    at_tail = ends[:, bonds:] + far
    apart = at_head - at_tail
    bond_old = apart[0:3]
    bond_new = apart[3:6]
    length = jnp.maximum(jnp.sqrt(jnp.sum(bond_old * bond_old, axis=0, keepdims=True)), 0.5)
    direction = bond_old / length
    mass_head, mass_tail = at_head[6:7], at_tail[6:7]
    scale = 1.0 / jnp.sqrt(mass_head + mass_tail)
    bent = scale * direction
    is_far = tail >= atoms
    near_mass = jnp.where(is_far, 0.0, mass_tail)
    right1 = scale * (jnp.sum(direction * bond_new, axis=0, keepdims=True) - length)

    col[...] = rows8([head, tail, mass_head, near_mass, bent]).T

    def couple_rows(i, carry):
        base = pl.multiple_of(i * step_rows, step_rows)
        block = col[pl.ds(base, step_rows), :]
        h, t, mh, mt = (block[:, k : k + 1] for k in range(4))
        same = h == head
        weight = jnp.where(same, mh, jnp.where(h == tail, -mh, 0.0)) + jnp.where(
            t == head, -mt, jnp.where(t == tail, mt, 0.0)
        )
        along = (
            block[:, 4:5] * bent[0:1] + block[:, 5:6] * bent[1:2] + block[:, 6:7] * bent[2:3]
        )
        entry = jnp.where(same, 1.0, 0.0) - along * weight
        high = entry.astype(BF16)
        a_high[pl.ds(base, step_rows), :] = high
        a_low[pl.ds(base, step_rows), :] = (entry - high.astype(F32)).astype(BF16)
        return carry

    lax.fori_loop(0, bonds // step_rows, couple_rows, 0)

    def couple(rows):
        high = rows.astype(BF16).astype(F32)
        both = jnp.concatenate([high, rows - high], axis=0).astype(BF16)
        out = dot_nn(both, a_high[...])
        count = rows.shape[0]
        return out[:count] + out[count:] + dot_nn(both, a_low[...])[:count]

    def to_slots(rows):
        return fold(dot_nn(pieces(rows), hot[bonds:, atoms:]))

    def to_bonds(rows):
        return fold(dot_nt(pieces(rows), hot[bonds:, atoms:]))

    mass_send = out0[6:7, :]

    def owner(terms, normal, response):
        moved, answers = [], []
        for k in range(ORDER + 1):
            here_k = terms[k]
            for i in range(k):
                gap = k - 1 - i
                here_k = here_k + (answers[i] if gap == 0 else response[gap - 1] * answers[i])
            total = rows8([jnp.sum(n * here_k, axis=0, keepdims=True) for n in normal])
            shift = send_count
            while shift < LANES:
                total = total + pltpu.roll(total, shift, 1)
                shift *= 2
            total = -mass_send * total
            moved.append(total[0:3])
            answers.append(sum(normal[d] * total[d : d + 1] for d in range(3)))
        return moved

    def finish(start, terms, injected):
        total = start
        for term in terms:
            total = total + term
        wave = injected[0:1]
        total = total + wave
        for k in range(1, ORDER):
            wave = couple(rows8([wave]))[0:1] + injected[k : k + 1]
            total = total + wave
        return total

    def local_series(rows):
        series = [rows]
        for _ in range(ORDER):
            series.append(couple(series[-1]))
        return series

    flags = jnp.where(is_far, 1.0, 0.0)
    series = local_series(rows8([right1, flags]))
    fixed = to_slots(rows8([bent] + [series[k][1:2] for k in range(1, ORDER)]))
    own_terms = to_slots(rows8([s[0:1] for s in series]))
    fill(out1, jnp.concatenate([fixed, own_terms], axis=0))
    second = copies_each(1, out1, in1)
    arrive(second)
    normal = [in1[:, k, :] for k in range(3)]
    response = [in1[:, 3 + k, :] for k in range(ORDER - 1)]
    moved1 = owner([in1[:, 8 + k, :] for k in range(ORDER + 1)], normal, response)
    sum1 = sum(moved1[1:], moved1[0])
    out2[...] = rows8(moved1[:ORDER] + [sum1])
    third = copies_same(2, out2, in2)
    arrive(third)

    def answer(rows):
        return [
            sum(fixed[d : d + 1] * rows[3 * k + d : 3 * k + d + 1] for d in range(3))
            for k in range(ORDER)
        ]

    seen = view(out2, in2)
    injected = to_bonds(rows8(answer(seen) + [seen[3 * ORDER : 3 * ORDER + 3]]))
    sol1 = finish(right1, [s[0:1] for s in series[1:]], injected)

    def spread(solution):
        pull = bent * solution
        both = jnp.concatenate([pull, -pull], axis=1)
        return mass * fold(dot_nn(pieces(rows8([both])), hot[:, :atoms]))[0:3]

    shift1 = spread(sol1)
    moved_ends = fold(dot_nt(pieces(rows8([shift1])), hot[:, :atoms]))[0:3]
    stretch = bond_new - (
        moved_ends[:, :bonds] - moved_ends[:, bonds:] - injected[ORDER : ORDER + 3]
    )
    current = jnp.sum(stretch * stretch, axis=0, keepdims=True)
    square = length * length
    goal = jnp.sqrt(jnp.maximum(2.0 * square - current, 0.5 * square))
    right2 = scale * (length - goal)
    series2 = local_series(rows8([right2]))
    fill(out3, to_slots(rows8([s[0:1] for s in series2])))
    fourth = copies_each(3, out3, in3)
    arrive(fourth)
    moved2 = owner([in3[:, k, :] for k in range(ORDER + 1)], normal, response)
    sum2 = sum(moved2[1:], moved2[0])
    out4[...] = rows8(moved2[:ORDER])
    fifth = copies_same(4, out4, in4)
    arrive(fifth)
    injected2 = to_bonds(rows8(answer(view(out4, in4))))
    sol2 = finish(right2, [s[0:1] for s in series2[1:]], injected2)

    once = jnp.where(lane_group == 0, sum1 + sum2, 0.0)
    at_send = fold(dot_nn(pieces(rows8([once])), pick[...]))[0:3]
    result = pos0 - shift1 - spread(sol2) - at_send
    for k in range(3):
        pos_ref[k, 0, 0] = result[k : k + 1]
    mult_ref[0, 0] = sol1 + sol2
    for copy in pending:
        copy.wait_send()


def per_device(axes, sizes, old_pos, displacement, inv_mass, bond_head, bond_tail, send_list):
    atoms, bonds, send_count = old_pos.shape[-1], bond_head.shape[-1], send_list.shape[-1]
    groups = LANES // send_count
    slots = -(-27 // groups) * LANES
    entries = plan(sizes, send_count)
    count = max(1, len(entries))
    same = max(1, len({where for where, _ in entries} - {(0, 0, 0)}))
    tile = lambda *shape: pltpu.VMEM(shape + (LANES,), F32)
    return pl.pallas_call(
        functools.partial(kernel, axes, sizes, send_count),
        out_shape=(
            jax.ShapeDtypeStruct(old_pos.shape, F32),
            jax.ShapeDtypeStruct(bond_head.shape, F32),
        ),
        in_specs=[pl.BlockSpec(memory_space=pltpu.VMEM)] * 6,
        out_specs=(pl.BlockSpec(memory_space=pltpu.VMEM), pl.BlockSpec(memory_space=pltpu.VMEM)),
        scratch_shapes=[
            pltpu.VMEM((2 * bonds, atoms + slots), BF16),
            pltpu.VMEM((LANES, atoms), BF16),
            pltpu.VMEM((bonds, bonds), BF16),
            pltpu.VMEM((bonds, bonds), BF16),
            pltpu.VMEM((bonds, 8), F32),
            tile(8), tile(same, 8),
            tile(count, 16), tile(count, 16),
            tile(16), tile(same, 16),
            tile(count, 8), tile(count, 8),
            tile(16), tile(same, 16),
            pltpu.SemaphoreType.DMA((5, count)),
            pltpu.SemaphoreType.DMA((5, count)),
        ],
        compiler_params=pltpu.CompilerParams(
            collective_id=0, has_side_effects=True, vmem_limit_bytes=56 * 1024 * 1024
        ),
    )(old_pos, displacement, inv_mass, bond_head, bond_tail, send_list)


def solution(mesh):
    axes = ("gx", "gy", "gz")
    sizes = tuple(mesh.shape[name] for name in axes)
    return jax.shard_map(
        functools.partial(per_device, axes, sizes),
        mesh=mesh,
        in_specs=(
            P(None, "gx", "gy", "gz", None),
            P(None, "gx", "gy", "gz", None),
            P("gx", "gy", "gz", None),
            P("gx", "gy", "gz", None),
            P("gx", "gy", "gz", None),
            P("gx", "gy", "gz", None),
        ),
        out_specs=(P(None, "gx", "gy", "gz", None), P("gx", "gy", "gz", None)),
        check_vma=False,
    )
```

time: 549 us -> 65.9 us (0.12); the launches traced: 541 us -> 65.6 us
  other arithmetic: 173 us -> 0 us
  starting transfers between devices: 149 us -> 0 us
  local copies, waits for them, and re-layouts: 114 us -> 1.93 us
  waiting for transfers between devices: 101 us -> 0 us
  Pallas kernels: 0 us -> 63.1 us
    scatter-add x30 -> x0, other arithmetic: 152 us -> none  [the longest x20 141 us: spread(): buffer.at[:, head_atom].add(weighted).at[:, tail_atom].add(-weighted)]
    ppermute x120 -> x0, starting transfers between devices: 149 us -> none  [the longest x60 88.1 us: with_halo(): after = lax.ppermute(leading, axis, down)]
    gather x46 -> x0, local copies, waits for them, and re-layouts: 102 us -> none  [the longest x8 32.1 us: couple(): extended[:, head_atom] - extended[:, tail_atom]]
    ppermute x120 -> x0, waiting for transfers between devices: 101 us -> none  [the longest x60 80.8 us: with_halo(): before = lax.ppermute(last, axis, up)]
    pallas_call x0 -> x1, Pallas kernels: none -> 63.1 us  [per_device(): pl.pallas_call(functools.partial(kernel, axes, sizes, send_count), out_sh...]
    reduce_sum x21 -> x0, other arithmetic: 9.59 us -> none  [the longest x8 7.33 us: couple(): jnp.sum(direction * (extended[:, head_atom] - extended[:, tail_atom]), ax...]
    concatenate x65 -> x0, other arithmetic: 6.08 us -> none  [the longest x8 4.37 us: couple(): jnp.concatenate([shift_vec, remote.reshape(3, wide_count)], axis=1)]
  transfers between devices with their start and end apart: 120 -> 0, of which waited for: 103 -> 0; matrix products, arithmetic and copies ran while one was open for 1% -> 0% of each run, Pallas kernels for 0% -> 0%
where the time goes in v1:
time: 65.9 us; the launch traced here: 65.6 us
  Pallas kernels  63.1 us (96%)
  local copies, waits for them, and re-layouts  1.93 us (3%)
    pallas_call x1, Pallas kernels, per_device(): pl.pallas_call(functools.partial(kernel, axes, sizes, send_count), out_sh...  63.1 us
    unnamed x4, local copies, waits for them, and re-layouts  1.93 us

profile of v1, /device:TPU:0, one launch (start us, length us, event | category | flops | bytes accessed | tf_op | source)
XLA Modules:
  0.0 65.6 jit_solution(8750371217680692953)
XLA Ops:
  0.6 63.1 %shard_map.77 = (f32[3,1,1,1,1536]{4,3,2,1,0:T(1,128)}, f32[1,1,1,1024]{3,2,1,0:T(1,128)}) custom-call(f32[3,1,1,1,1536]{4,3,2,1,0:T(1,128)} %old_ref.1, f32[3,1,1,1,1536]{4,3,2,1,0:T(1,128)} %move_ref.1, f32[1,1,1,1536]{3,2,1,0:T(1,128)} %mass_ref.1, s32[1,1,1,1024]{3,2,1,0:T(1,128)} %head_ref.1, s32[1,1,1,1024]{3,2,1,0:T(1,128)} %tail_ref.1, ...), custom_call_target="tpu_custom_call" | custom-call | tf_op jit(solution)/shard_map/pallas_call | solution.py:343
  63.7 0.0 copy-start
  63.7 1.3 %copy.10 = f32[3,1,1,1,1536]{4,3,2,1,0:T(1,128)} copy(f32[3,1,1,1,1536]{4,3,2,1,0:T(1,128)} %get-tuple-element.4) | data formatting | bytes 36864
  65.0 0.0 copy-done
  65.0 0.6 copy.11
Async XLA Ops:
  63.7 1.3 %copy-start = (f32[1,1,1,1024]{3,2,1,0:T(1,128)S(1)}, f32[1,1,1,1024]{3,2,1,0:T(1,128)}, u32[]{:S(2)}) copy-start(f32[1,1,1,1024]{3,2,1,0:T(1,128)} %get-tuple-element.5) | copy-start | bytes 12292

commit v2 on v1

--- a/solution.py
+++ b/solution.py
@@ -63,7 +63,7 @@
     axes, sizes, send_count,
     old_ref, move_ref, mass_ref, head_ref, tail_ref, send_ref,
     pos_ref, mult_ref,
-    hot, pick, a_high, a_low, col,
+    hot_head, ends, pick, above, beside, root, col,
     out0, in0, out1, in1, out2, in2, out3, in3, out4, in4,
     send_sem, recv_sem,
 ):
@@ -173,67 +173,85 @@
     wide_lane = lax.broadcasted_iota(jnp.int32, (1, atoms + slots), 1).astype(F32)
     step_rows = 16
 
-    def hot_rows(i, carry):
+    def index_rows(i, carry):
         base = pl.multiple_of(i * step_rows, step_rows)
         block = col[pl.ds(base, step_rows), :]
-        hot[pl.ds(base, step_rows), :] = jnp.where(block[:, 0:1] == wide_lane, 1.0, 0.0).astype(BF16)
-        hot[pl.ds(bonds + base, step_rows), :] = jnp.where(
-            block[:, 1:2] == wide_lane, 1.0, 0.0
+        h, t = block[:, 0:1], block[:, 1:2]
+        at_h = h == atom_lane
+        hot_head[pl.ds(base, step_rows), :] = jnp.where(at_h, 1.0, 0.0).astype(BF16)
+        ends[pl.ds(base, step_rows), :] = jnp.where(
+            h == wide_lane, 1.0, jnp.where(t == wide_lane, -1.0, 0.0)
+        ).astype(BF16)
+        above[pl.ds(base, step_rows), :] = jnp.where(t == head, 1.0, 0.0).astype(BF16)
+        beside[pl.ds(base, step_rows), :] = jnp.where(
+            t == tail, 1.0, jnp.where(h == tail, -1.0, 0.0)
         ).astype(BF16)
         return carry
 
-    lax.fori_loop(0, bonds // step_rows, hot_rows, 0)
-    ends = fold(dot_nt(values, hot[:, :atoms]))
+    lax.fori_loop(0, bonds // step_rows, index_rows, 0)
+    apart = fold(dot_nt(values, ends[:, :atoms]))
+    mass_head = fold(dot_nt(pieces(rows8([mass])), hot_head[...]))[0:1]
+    is_far = tail >= atoms
+    flags = jnp.where(is_far, 1.0, 0.0)
+
+    def climb(label):
+        rows = jnp.broadcast_to(label, (8, bonds))
+        high = rows.astype(BF16).astype(F32)
+        both = jnp.concatenate([high, rows - high], axis=0).astype(BF16)
+        out = dot_nt(both, above[...])
+        return jnp.where(is_far, tail, out[0:1] + out[8:9])
+
+    def mark(label):
+        col[:, 0:8] = jnp.broadcast_to(label, (8, bonds)).T
+        slot_lane = (lax.broadcasted_iota(jnp.int32, (1, slots), 1) + atoms).astype(F32)
+
+        def mark_rows(i, carry):
+            base = pl.multiple_of(i * 32, 32)
+            block = col[pl.ds(base, 32), :]
+            root[pl.ds(base, 32), :] = jnp.where(block[:, 0:1] == slot_lane, 1.0, 0.0).astype(BF16)
+            return carry
+
+        lax.fori_loop(0, bonds // 32, mark_rows, 0)
+
+    label = jnp.where(is_far, tail, 0.0)
+    for _ in range(ORDER // 2):
+        label = climb(label)
+    mark(label)
 
     arrive(first)
-    far = fold(dot_nt(pieces(view(out0, in0)), hot[bonds:, atoms:]))
-    at_head = ends[:, :bonds]
-    at_tail = ends[:, bonds:] + far
-    apart = at_head - at_tail
+    apart = apart + fold(dot_nt(pieces(view(out0, in0)), ends[:, atoms:]))
     bond_old = apart[0:3]
     bond_new = apart[3:6]
     length = jnp.maximum(jnp.sqrt(jnp.sum(bond_old * bond_old, axis=0, keepdims=True)), 0.5)
     direction = bond_old / length
-    mass_head, mass_tail = at_head[6:7], at_tail[6:7]
+    mass_tail = mass_head - apart[6:7]
     scale = 1.0 / jnp.sqrt(mass_head + mass_tail)
     bent = scale * direction
-    is_far = tail >= atoms
     near_mass = jnp.where(is_far, 0.0, mass_tail)
     right1 = scale * (jnp.sum(direction * bond_new, axis=0, keepdims=True) - length)
 
-    col[...] = rows8([head, tail, mass_head, near_mass, bent]).T
-
-    def couple_rows(i, carry):
-        base = pl.multiple_of(i * step_rows, step_rows)
-        block = col[pl.ds(base, step_rows), :]
-        h, t, mh, mt = (block[:, k : k + 1] for k in range(4))
-        same = h == head
-        weight = jnp.where(same, mh, jnp.where(h == tail, -mh, 0.0)) + jnp.where(
-            t == head, -mt, jnp.where(t == tail, mt, 0.0)
-        )
-        along = (
-            block[:, 4:5] * bent[0:1] + block[:, 5:6] * bent[1:2] + block[:, 6:7] * bent[2:3]
-        )
-        entry = jnp.where(same, 1.0, 0.0) - along * weight
-        high = entry.astype(BF16)
-        a_high[pl.ds(base, step_rows), :] = high
-        a_low[pl.ds(base, step_rows), :] = (entry - high.astype(F32)).astype(BF16)
-        return carry
-
-    lax.fori_loop(0, bonds // step_rows, couple_rows, 0)
-
-    def couple(rows):
+    def meet(pull):
+        rows = rows8([pull])
+        count = rows.shape[0]
         high = rows.astype(BF16).astype(F32)
         both = jnp.concatenate([high, rows - high], axis=0).astype(BF16)
-        out = dot_nn(both, a_high[...])
-        count = rows.shape[0]
-        return out[:count] + out[count:] + dot_nn(both, a_low[...])[:count]
+        up = dot_nn(both, above[...])
+        side = dot_nn(both, beside[...])
+        out = mass_head * (rows - up[:count] - up[count:]) + near_mass * (side[:count] + side[count:])
+        return out[: pull.shape[0]]
+
+    def couple(*rows):
+        out = meet(jnp.concatenate([bent * row for row in rows], axis=0))
+        return [
+            row - jnp.sum(bent * out[3 * k : 3 * k + 3], axis=0, keepdims=True)
+            for k, row in enumerate(rows)
+        ]
 
     def to_slots(rows):
-        return fold(dot_nn(pieces(rows), hot[bonds:, atoms:]))
+        return fold(dot_nn(pieces(rows8(rows)), root[...]))
 
     def to_bonds(rows):
-        return fold(dot_nt(pieces(rows), hot[bonds:, atoms:]))
+        return fold(dot_nt(pieces(rows8(rows)), root[...]))
 
     mass_send = out0[6:7, :]
 
@@ -254,29 +272,35 @@
             answers.append(sum(normal[d] * total[d : d + 1] for d in range(3)))
         return moved
 
-    def finish(start, terms, injected):
-        total = start
-        for term in terms:
-            total = total + term
-        wave = injected[0:1]
-        total = total + wave
-        for k in range(1, ORDER):
-            wave = couple(rows8([wave]))[0:1] + injected[k : k + 1]
-            total = total + wave
+    def through(injected):
+        total = 0.0
+        weight = 0.0
+        for k in range(ORDER):
+            weight = weight + far_terms[k]
+            total = total + weight * injected[ORDER - 1 - k : ORDER - k]
         return total
 
-    def local_series(rows):
-        series = [rows]
-        for _ in range(ORDER):
-            series.append(couple(series[-1]))
-        return series
-
-    flags = jnp.where(is_far, 1.0, 0.0)
-    series = local_series(rows8([right1, flags]))
-    fixed = to_slots(rows8([bent] + [series[k][1:2] for k in range(1, ORDER)]))
-    own_terms = to_slots(rows8([s[0:1] for s in series]))
+    terms1, far_terms = [right1], [flags]
+    half = ORDER // 2
+    for _ in range(half):
+        near, far = couple(terms1[-1], far_terms[-1])
+        terms1.append(near)
+        far_terms.append(far)
+
+    def at_far(terms, k):
+        return far_terms[max(0, k - half)] * terms[min(k, half)]
+
+    fixed = to_slots([bent * flags] + [at_far(far_terms, k) for k in range(1, ORDER)])
+    own_terms = to_slots([at_far(terms1, k) for k in range(ORDER + 1)])
     fill(out1, jnp.concatenate([fixed, own_terms], axis=0))
     second = copies_each(1, out1, in1)
+    for _ in range(ORDER - half):
+        near, far = couple(terms1[-1], far_terms[-1])
+        terms1.append(near)
+        far_terms.append(far)
+        label = climb(label)
+    mark(label)
+    base1 = sum(terms1[1:], terms1[0])
     arrive(second)
     normal = [in1[:, k, :] for k in range(3)]
     response = [in1[:, 3 + k, :] for k in range(ORDER - 1)]
@@ -293,41 +317,35 @@
         ]
 
     seen = view(out2, in2)
-    injected = to_bonds(rows8(answer(seen) + [seen[3 * ORDER : 3 * ORDER + 3]]))
-    sol1 = finish(right1, [s[0:1] for s in series[1:]], injected)
-
-    def spread(solution):
-        pull = bent * solution
-        both = jnp.concatenate([pull, -pull], axis=1)
-        return mass * fold(dot_nn(pieces(rows8([both])), hot[:, :atoms]))[0:3]
-
-    shift1 = spread(sol1)
-    moved_ends = fold(dot_nt(pieces(rows8([shift1])), hot[:, :atoms]))[0:3]
-    stretch = bond_new - (
-        moved_ends[:, :bonds] - moved_ends[:, bonds:] - injected[ORDER : ORDER + 3]
-    )
+    injected = to_bonds(answer(seen) + [seen[3 * ORDER : 3 * ORDER + 3]])
+    sol1 = base1 + through(injected)
+    stretch = bond_new - (meet(bent * sol1) - flags * injected[ORDER : ORDER + 3])
     current = jnp.sum(stretch * stretch, axis=0, keepdims=True)
     square = length * length
     goal = jnp.sqrt(jnp.maximum(2.0 * square - current, 0.5 * square))
     right2 = scale * (length - goal)
-    series2 = local_series(rows8([right2]))
-    fill(out3, to_slots(rows8([s[0:1] for s in series2])))
+    fill(out3, to_slots([far_terms[k] * right2 for k in range(ORDER + 1)]))
     fourth = copies_each(3, out3, in3)
+    term, both = right2, sol1 + right2
+    for _ in range(half):
+        (term,) = couple(term)
+        both = both + term
     arrive(fourth)
     moved2 = owner([in3[:, k, :] for k in range(ORDER + 1)], normal, response)
     sum2 = sum(moved2[1:], moved2[0])
     out4[...] = rows8(moved2[:ORDER])
     fifth = copies_same(4, out4, in4)
+    for _ in range(ORDER - half):
+        (term,) = couple(term)
+        both = both + term
+    once = jnp.where(lane_group == 0, sum1 + sum2, 0.0)
+    start = pos0 - fold(dot_nn(pieces(rows8([once])), pick[...]))[0:3]
     arrive(fifth)
-    injected2 = to_bonds(rows8(answer(view(out4, in4))))
-    sol2 = finish(right2, [s[0:1] for s in series2[1:]], injected2)
-
-    once = jnp.where(lane_group == 0, sum1 + sum2, 0.0)
-    at_send = fold(dot_nn(pieces(rows8([once])), pick[...]))[0:3]
-    result = pos0 - shift1 - spread(sol2) - at_send
+    both = both + through(to_bonds(answer(view(out4, in4))))
+    mult_ref[0, 0] = both
+    result = start - mass * fold(dot_nn(pieces(rows8([bent * both])), ends[:, :atoms]))[0:3]
     for k in range(3):
         pos_ref[k, 0, 0] = result[k : k + 1]
-    mult_ref[0, 0] = sol1 + sol2
     for copy in pending:
         copy.wait_send()
 
@@ -349,10 +367,12 @@
         in_specs=[pl.BlockSpec(memory_space=pltpu.VMEM)] * 6,
         out_specs=(pl.BlockSpec(memory_space=pltpu.VMEM), pl.BlockSpec(memory_space=pltpu.VMEM)),
         scratch_shapes=[
-            pltpu.VMEM((2 * bonds, atoms + slots), BF16),
+            pltpu.VMEM((bonds, atoms), BF16),
+            pltpu.VMEM((bonds, atoms + slots), BF16),
             pltpu.VMEM((LANES, atoms), BF16),
             pltpu.VMEM((bonds, bonds), BF16),
             pltpu.VMEM((bonds, bonds), BF16),
+            pltpu.VMEM((bonds, slots), BF16),
             pltpu.VMEM((bonds, 8), F32),
             tile(8), tile(same, 8),
             tile(count, 16), tile(count, 16),

time: 65.9 us -> 53.6 us (0.81)
  Pallas kernels: 63.1 us -> 50.8 us
    pallas_call x1, Pallas kernels: 63.1 us -> 50.8 us  [per_device(): pl.pallas_call(functools.partial(kernel, axes, sizes, send_count), out_sh...]
where the time goes in v2:
time: 53.6 us; the launch traced here: 53.4 us
  Pallas kernels  50.8 us (95%)
  local copies, waits for them, and re-layouts  1.93 us (4%)
  between operations  0.65 us (1%)
    pallas_call x1, Pallas kernels, per_device(): pl.pallas_call(functools.partial(kernel, axes, sizes, send_count), out_sh...  50.8 us
    unnamed x4, local copies, waits for them, and re-layouts  1.93 us

profile of v2, /device:TPU:0, one launch (start us, length us, event | category | flops | bytes accessed | tf_op | source)
XLA Modules:
  0.0 53.4 jit_solution(11563588651437606310)
XLA Ops:
  0.6 50.8 %shard_map.77 = (f32[3,1,1,1,1536]{4,3,2,1,0:T(1,128)}, f32[1,1,1,1024]{3,2,1,0:T(1,128)}) custom-call(f32[3,1,1,1,1536]{4,3,2,1,0:T(1,128)} %old_ref.1, f32[3,1,1,1,1536]{4,3,2,1,0:T(1,128)} %move_ref.1, f32[1,1,1,1536]{3,2,1,0:T(1,128)} %mass_ref.1, s32[1,1,1,1024]{3,2,1,0:T(1,128)} %head_ref.1, s32[1,1,1,1024]{3,2,1,0:T(1,128)} %tail_ref.1, ...), custom_call_target="tpu_custom_call" | custom-call | tf_op jit(solution)/shard_map/pallas_call | solution.py:361
  51.5 0.0 copy-start
  51.5 1.3 %copy.10 = f32[3,1,1,1,1536]{4,3,2,1,0:T(1,128)} copy(f32[3,1,1,1,1536]{4,3,2,1,0:T(1,128)} %get-tuple-element.4) | data formatting | bytes 36864
  52.8 0.0 copy-done
  52.8 0.6 %copy.11 = f32[1,1,1,1024]{3,2,1,0:T(1,128)} copy(f32[1,1,1,1024]{3,2,1,0:T(1,128)S(1)} %copy-done) | data formatting | bytes 8192
Async XLA Ops:
  51.5 1.3 %copy-start = (f32[1,1,1,1024]{3,2,1,0:T(1,128)S(1)}, f32[1,1,1,1024]{3,2,1,0:T(1,128)}, u32[]{:S(2)}) copy-start(f32[1,1,1,1024]{3,2,1,0:T(1,128)} %get-tuple-element.5) | copy-start | bytes 12292

commit v3 on v2

--- a/solution.py
+++ b/solution.py
@@ -63,7 +63,7 @@
     axes, sizes, send_count,
     old_ref, move_ref, mass_ref, head_ref, tail_ref, send_ref,
     pos_ref, mult_ref,
-    hot_head, ends, pick, above, beside, root, col,
+    low, pick, above, beside, root, col,
     out0, in0, out1, in1, out2, in2, out3, in3, out4, in4,
     send_sem, recv_sem,
 ):
@@ -101,8 +101,8 @@
     old = jnp.concatenate([old_ref[k, 0, 0] for k in range(3)], axis=0)
     pos0 = old + jnp.concatenate([move_ref[k, 0, 0] for k in range(3)], axis=0)
     mass = mass_ref[0, 0]
-    values = pieces(rows8([old, pos0, mass]))
-    out0[...] = fold(dot_nt(values, pick[...]))
+    data = rows8([old, pos0, mass])
+    out0[...] = fold(dot_nt(pieces(data), pick[...]))
 
     if devices:
         pl.semaphore_wait(barrier, len(devices))
@@ -169,18 +169,21 @@
 
     head = head_ref[0, 0].astype(F32)
     tail = tail_ref[0, 0].astype(F32)
-    col[...] = rows8([head, tail]).T
-    wide_lane = lax.broadcasted_iota(jnp.int32, (1, atoms + slots), 1).astype(F32)
+    end_atom = jnp.concatenate([head_ref[0, 0], tail_ref[0, 0]], axis=1)
+    end_tile = (end_atom // LANES).astype(F32)
+    end_lane = (end_atom % LANES).astype(F32)
+    col[...] = rows8([head, tail, end_lane[:, :bonds], end_lane[:, bonds:]]).T
+    one_lane = lax.broadcasted_iota(jnp.int32, (1, LANES), 1).astype(F32)
+    atom_tiles = atoms // LANES
     step_rows = 16
 
     def index_rows(i, carry):
         base = pl.multiple_of(i * step_rows, step_rows)
         block = col[pl.ds(base, step_rows), :]
         h, t = block[:, 0:1], block[:, 1:2]
-        at_h = h == atom_lane
-        hot_head[pl.ds(base, step_rows), :] = jnp.where(at_h, 1.0, 0.0).astype(BF16)
-        ends[pl.ds(base, step_rows), :] = jnp.where(
-            h == wide_lane, 1.0, jnp.where(t == wide_lane, -1.0, 0.0)
+        low[pl.ds(base, step_rows), :] = jnp.where(block[:, 2:3] == one_lane, 1.0, 0.0).astype(BF16)
+        low[pl.ds(bonds + base, step_rows), :] = jnp.where(
+            block[:, 3:4] == one_lane, 1.0, 0.0
         ).astype(BF16)
         above[pl.ds(base, step_rows), :] = jnp.where(t == head, 1.0, 0.0).astype(BF16)
         beside[pl.ds(base, step_rows), :] = jnp.where(
@@ -189,8 +192,19 @@
         return carry
 
     lax.fori_loop(0, bonds // step_rows, index_rows, 0)
-    apart = fold(dot_nt(values, ends[:, :atoms]))
-    mass_head = fold(dot_nt(pieces(rows8([mass])), hot_head[...]))[0:1]
+
+    def take(rows, hot, where, base):
+        tiles = rows.shape[1] // LANES
+        stacked = jnp.concatenate(
+            [rows[:, k * LANES : (k + 1) * LANES] for k in range(tiles)], axis=0
+        )
+        found = fold(dot_nt(pieces(stacked), hot))
+        total = jnp.zeros((8, hot.shape[0]), F32)
+        for k in range(tiles):
+            total = jnp.where(where == base + k, found[8 * k : 8 * k + 8], total)
+        return total
+
+    at_ends = take(data, low[...], end_tile, 0)
     is_far = tail >= atoms
     flags = jnp.where(is_far, 1.0, 0.0)
 
@@ -219,12 +233,15 @@
     mark(label)
 
     arrive(first)
-    apart = apart + fold(dot_nt(pieces(view(out0, in0)), ends[:, atoms:]))
+    at_tail = at_ends[:, bonds:] + take(
+        view(out0, in0), low[bonds:, :], end_tile[:, bonds:], atom_tiles
+    )
+    apart = at_ends[:, :bonds] - at_tail
+    mass_head, mass_tail = at_ends[6:7, :bonds], at_tail[6:7]
     bond_old = apart[0:3]
     bond_new = apart[3:6]
     length = jnp.maximum(jnp.sqrt(jnp.sum(bond_old * bond_old, axis=0, keepdims=True)), 0.5)
     direction = bond_old / length
-    mass_tail = mass_head - apart[6:7]
     scale = 1.0 / jnp.sqrt(mass_head + mass_tail)
     bent = scale * direction
     near_mass = jnp.where(is_far, 0.0, mass_tail)
@@ -294,13 +311,16 @@
     own_terms = to_slots([at_far(terms1, k) for k in range(ORDER + 1)])
     fill(out1, jnp.concatenate([fixed, own_terms], axis=0))
     second = copies_each(1, out1, in1)
-    for _ in range(ORDER - half):
-        near, far = couple(terms1[-1], far_terms[-1])
-        terms1.append(near)
-        far_terms.append(far)
-        label = climb(label)
-    mark(label)
-    base1 = sum(terms1[1:], terms1[0])
+
+    def longer(steps, label):
+        for _ in range(steps):
+            near, far = couple(terms1[-1], far_terms[-1])
+            terms1.append(near)
+            far_terms.append(far)
+            label = climb(label)
+        return label
+
+    label = longer((ORDER - half) // 2, label)
     arrive(second)
     normal = [in1[:, k, :] for k in range(3)]
     response = [in1[:, 3 + k, :] for k in range(ORDER - 1)]
@@ -308,6 +328,8 @@
     sum1 = sum(moved1[1:], moved1[0])
     out2[...] = rows8(moved1[:ORDER] + [sum1])
     third = copies_same(2, out2, in2)
+    mark(longer(ORDER - half - (ORDER - half) // 2, label))
+    base1 = sum(terms1[1:], terms1[0])
     arrive(third)
 
     def answer(rows):
@@ -343,7 +365,16 @@
     arrive(fifth)
     both = both + through(to_bonds(answer(view(out4, in4))))
     mult_ref[0, 0] = both
-    result = start - mass * fold(dot_nn(pieces(rows8([bent * both])), ends[:, :atoms]))[0:3]
+    pull = bent * both
+    parts = pieces(rows8([jnp.concatenate([pull, -pull], axis=1)])).astype(F32)
+    kept = jnp.concatenate(
+        [jnp.where(end_tile == k, parts, 0.0) for k in range(atom_tiles)], axis=0
+    )
+    added = dot_nn(kept.astype(BF16), low[...])
+    added = jnp.concatenate(
+        [fold(added[24 * k : 24 * k + 24]) for k in range(atom_tiles)], axis=1
+    )
+    result = start - mass * added[0:3]
     for k in range(3):
         pos_ref[k, 0, 0] = result[k : k + 1]
     for copy in pending:
@@ -367,8 +398,7 @@
         in_specs=[pl.BlockSpec(memory_space=pltpu.VMEM)] * 6,
         out_specs=(pl.BlockSpec(memory_space=pltpu.VMEM), pl.BlockSpec(memory_space=pltpu.VMEM)),
         scratch_shapes=[
-            pltpu.VMEM((bonds, atoms), BF16),
-            pltpu.VMEM((bonds, atoms + slots), BF16),
+            pltpu.VMEM((2 * bonds, LANES), BF16),
             pltpu.VMEM((LANES, atoms), BF16),
             pltpu.VMEM((bonds, bonds), BF16),
             pltpu.VMEM((bonds, bonds), BF16),

time: 53.6 us -> 50.7 us (0.946)
  Pallas kernels: 50.8 us -> 47.9 us
    pallas_call x1, Pallas kernels: 50.8 us -> 47.9 us  [per_device(): pl.pallas_call(functools.partial(kernel, axes, sizes, send_count), out_sh...]
where the time goes in v3:
time: 50.7 us; the launch traced here: 50.5 us
  Pallas kernels  47.9 us (94%)
  local copies, waits for them, and re-layouts  1.93 us (4%)
  between operations  0.65 us (1%)
    pallas_call x1, Pallas kernels, per_device(): pl.pallas_call(functools.partial(kernel, axes, sizes, send_count), out_sh...  47.9 us
    unnamed x4, local copies, waits for them, and re-layouts  1.93 us

profile of v3, /device:TPU:0, one launch (start us, length us, event | category | flops | bytes accessed | tf_op | source)
XLA Modules:
  0.0 50.5 jit_solution(14873629037271392048)
XLA Ops:
  0.6 47.9 %shard_map.77 = (f32[3,1,1,1,1536]{4,3,2,1,0:T(1,128)}, f32[1,1,1,1024]{3,2,1,0:T(1,128)}) custom-call(f32[3,1,1,1,1536]{4,3,2,1,0:T(1,128)} %old_ref.1, f32[3,1,1,1,1536]{4,3,2,1,0:T(1,128)} %move_ref.1, f32[1,1,1,1536]{3,2,1,0:T(1,128)} %mass_ref.1, s32[1,1,1,1024]{3,2,1,0:T(1,128)} %head_ref.1, s32[1,1,1,1024]{3,2,1,0:T(1,128)} %tail_ref.1, ...), custom_call_target="tpu_custom_call" | custom-call | tf_op jit(solution)/shard_map/pallas_call | solution.py:392
  48.5 0.0 copy-start
  48.5 1.3 %copy.10 = f32[3,1,1,1,1536]{4,3,2,1,0:T(1,128)} copy(f32[3,1,1,1,1536]{4,3,2,1,0:T(1,128)} %get-tuple-element.4) | data formatting | bytes 36864
  49.9 0.0 copy-done
  49.9 0.6 %copy.11 = f32[1,1,1,1024]{3,2,1,0:T(1,128)} copy(f32[1,1,1,1024]{3,2,1,0:T(1,128)S(1)} %copy-done) | data formatting | bytes 8192
Async XLA Ops:
  48.5 1.3 %copy-start = (f32[1,1,1,1024]{3,2,1,0:T(1,128)S(1)}, f32[1,1,1,1024]{3,2,1,0:T(1,128)}, u32[]{:S(2)}) copy-start(f32[1,1,1,1024]{3,2,1,0:T(1,128)} %get-tuple-element.5) | copy-start | bytes 12292
